TPU v7x, 32 devices: a whole 2x2x4 slice. The times are simulated.
32 devices in a mesh: groups: 2 (over x), pts: 8 (over z, y), lm: 2 (over core).
Axes of the slice: x: 2, y: 2, z: 4, core: 2. Of those that a mesh axis runs over, the one named last changes fastest.
Arguments:
- points: float32 [3, 4096], P(None, ('groups', 'pts', 'lm')), parts along dimension 1, may hold values from 0 to 1, as said below
- targets: float32 [32, 4096], P(None, ('groups', 'pts', 'lm')), parts along dimension 1, may hold values from -12 to 12
- order: int32 [4096], P(('groups', 'pts', 'lm')), parts along dimension 0, may hold values from 0 to 2047, as said below
- landmarks: int32 [2048], P('groups'), parts along dimension 0, may hold values from 0 to 2047, as said below
Outputs:
- coefficients: float32 [32, 4096], P(None, ('groups', 'pts', 'lm')), parts along dimension 1
- residual: float32 [32, 4096], P(None, ('groups', 'pts', 'lm')), parts along dimension 1
There are 2 independent parts, one for each index of `groups`. A program takes and returns all parts, laid end to end along the dimension named above; each array names one. Nothing has to cross between parts.
Inputs may be any that keep to these rules, and one draw needn't show every extreme that they name: Each column is a point of the unit cube. Points are stored in Z-order: the 128 points of each aligned block of columns lie in one box of a regular grid, and consecutive blocks follow the Z-order curve through the boxes. `order`: A permutation of 0 to 2047. `landmarks`: 1024 distinct point indices.
All inputs are finite; a program needn't handle non-finite values.
Results may differ from a plain program's by a relative error of at most 0.0003.
Values sent between devices are 32-bit elements; how exact they have to be, the bound alone decides.
No kernel may reach another device: no remote copies, remote signals or barrier semaphores. Data moves between devices by JAX's collectives and lax.ppermute only.
A program may use at most 128 MiB of HBM per device.

v0:
```python
import math
import jax
import jax.numpy as jnp
from jax import lax
from jax.sharding import PartitionSpec as P

ITERS = 2
root_five = 2.23606797749979
signal_var = 0.1
inverse_square_length = 25.0
highest = lax.Precision.HIGHEST


def matern(near, far):
    first = near[0][:, None] - far[0][None, :]
    second = near[1][:, None] - far[1][None, :]
    third = near[2][:, None] - far[2][None, :]
    scaled = (first * first + second * second + third * third) * inverse_square_length
    reach = jnp.sqrt(scaled)
    return signal_var * (1.0 + root_five * reach + 5.0 / 3.0 * scaled) * jnp.exp(-root_five * reach)


def tile_product(near, piece):
    width = piece.shape[1]
    block = math.gcd(width, 512)

    def accumulate(index, total):
        slab = lax.dynamic_slice_in_dim(piece, index * block, block, 1)
        return total + jnp.dot(slab[3:], matern(slab[:3], near), precision=highest)

    empty = jnp.zeros((piece.shape[0] - 3, near.shape[1]), jnp.float32)
    return lax.fori_loop(0, width // block, accumulate, empty)


def landmark_total(vector, cross):
    return lax.psum(jnp.dot(vector, cross, precision=highest), ("pts", "lm"))


def body(points, targets, order, landmarks):
    rows = points.shape[1]
    count = landmarks.shape[0]
    offset = lax.axis_index(("pts", "lm")) * rows
    every = lax.all_gather(targets, ("pts", "lm"), axis=1, tiled=True)
    goal = jnp.take(every, order, axis=1)
    local = landmarks - offset
    inside = (local >= 0) & (local < rows)
    picked = jnp.where(inside[None, :], jnp.take(points, jnp.clip(local, 0, rows - 1), axis=1), 0.0)
    anchors = lax.psum(picked, ("pts", "lm"))
    cross = matern(points, anchors)
    gram = lax.psum(jnp.einsum("ri,rj->ij", cross, cross, precision=highest), ("pts", "lm"))
    inner = matern(anchors, anchors) + jnp.eye(count, dtype=jnp.float32) + gram
    factor = jnp.linalg.cholesky(inner)
    solution = jnp.zeros_like(goal)
    residual = goal
    summed = landmark_total(residual, cross)
    for step in range(ITERS):
        weights = jax.scipy.linalg.cho_solve((factor, True), summed.T)
        scaled_res = residual - jnp.dot(cross, weights, precision=highest).T
        stacked = jnp.concatenate([points, scaled_res], axis=0)
        image = (
            tile_product(points, lax.all_gather(stacked, ("pts", "lm"), axis=1, tiled=True))
            + scaled_res
        )
        current, curvature, lifted = lax.psum(
            (
                jnp.sum(residual * scaled_res, axis=1),
                jnp.sum(scaled_res * image, axis=1),
                jnp.dot(image, cross, precision=highest),
            ),
            ("pts", "lm"),
        )
        if step == 0:
            stride = current / curvature
            direction = scaled_res
            along = image
            along_lift = lifted
        else:
            ratio = current / previous
            stride = current / (curvature - ratio * current / stride)
            direction = scaled_res + ratio[:, None] * direction
            along = image + ratio[:, None] * along
            along_lift = lifted + ratio[:, None] * along_lift
        solution = solution + stride[:, None] * direction
        residual = residual - stride[:, None] * along
        summed = summed - stride[:, None] * along_lift
        previous = current
    return (solution, residual)


def solution(mesh):
    return jax.shard_map(
        body,
        mesh=mesh,
        in_specs=(
            P(None, ("groups", "pts", "lm")),
            P(None, ("groups", "pts", "lm")),
            P(("groups", "pts", "lm")),
            P("groups"),
        ),
        out_specs=(P(None, ("groups", "pts", "lm")), P(None, ("groups", "pts", "lm"))),
        check_vma=False,
    )
```

profile of v0, /device:TPU:0, one launch (start us, length us, event | category | flops | bytes accessed | tf_op | source)
XLA Modules:
  0.0 779.8 jit_solution(6662976577567026140)
XLA Ops:
  11.5 2.8 gather_fusion.1
  14.7 68.3 %psum.56 = f32[3,1024]{0,1:T(8,128)S(1)} all-reduce(f32[3,1024]{0,1:T(8,128)S(1)} %select_bitcast_fusion), channel_id=1, replica_groups=mesh['groups'=2,'pts'=8,'lm'=2] {'pts','lm'}, use_global_device_ids=true, to_apply=%region_0.1 | all-reduce | flops 3072 | bytes 24576 | tf_op jit(solution)/shard_map/psum | solution.py:48
  84.6 21.3 %all_gather.9 = f32[32,2048]{0,1:T(8,128)S(1)} all-gather(f32[32,128]{0,1:T(8,128)S(1)} %copy.11), channel_id=1, replica_groups=mesh['groups'=2,'pts'=8,'lm'=2] {'pts','lm'}, dimensions={1}, use_global_device_ids=true | all-gather | bytes 278528 | tf_op jit(solution)/shard_map/all_gather | solution.py:43
  106.6 6.6 fusion.103
  113.2 1.6 fusion.102
  114.9 112.6 %all-reduce.9.cloned.1.call-done = (f32[1024,1024]{0,1:T(8,128)}, f32[32,1024]{1,0:T(8,128)}) async-done(((f32[1024,1024]{0,1:T(8,128)}, f32[32,1024]{1,0:T(8,128)}), (f32[1024,1024]{0,1:T(8,128)}, f32[32,1024]{1,0:T(8,128)})) %all-reduce.9.cloned.1.call-update) | async-done | bytes 4325392 | tf_op jit(solution)/shard_map/psum | solution.py:50
  227.5 7.6 add_add_fusion
  235.1 5.3 copy.15
  240.5 7.4 fusion.74
  247.8 1.9 copy-done
  249.8 11.7 %cholesky.223 = f32[128,128]{1,0:T(8,128)S(1)} custom-call(f32[128,128]{1,0:T(8,128)S(1)} %cholesky.580), custom_call_target="Cholesky" | custom-call | tf_op jit(solution)/shard_map/jit(cholesky)/cholesky | solution.py:52
  261.5 2.5 cholesky.255
  264.0 9.8 %custom-call.64 = f32[1,128,128]{1,2,0:T(8,128)S(1)} custom-call(f32[1,128,128]{2,1,0:T(8,128)S(1)} %get-tuple-element.346), custom_call_target="InvertDiagBlocksLowerTriangular" | custom-call | tf_op jit(solution)/shard_map/jit(cholesky)/cholesky | solution.py:52
  273.8 2.4 constant_dynamic-update-slice_fusion.93
  276.2 1.5 convolution_subtract_fusion
  277.8 11.7 %cholesky.244 = f32[128,128]{1,0:T(8,128)S(1)} custom-call(f32[128,128]{1,0:T(8,128)S(1)} %cholesky.584), custom_call_target="Cholesky" | custom-call | tf_op jit(solution)/shard_map/jit(cholesky)/cholesky | solution.py:52
  290.1 10.0 %custom-call.65 = f32[1,128,128]{1,2,0:T(8,128)S(1)} custom-call(f32[1,128,128]{2,1,0:T(8,128)S(1)} %get-tuple-element.343), custom_call_target="InvertDiagBlocksLowerTriangular" | custom-call | tf_op jit(solution)/shard_map/jit(cholesky)/cholesky | solution.py:52
  301.4 2.1 convolution_subtract_fusion.1
  303.5 11.7 %cholesky.468 = f32[128,128]{1,0:T(8,128)S(1)} custom-call(f32[128,128]{1,0:T(8,128)S(1)} %cholesky.589), custom_call_target="Cholesky" | custom-call | tf_op jit(solution)/shard_map/jit(cholesky)/cholesky | solution.py:52
  316.4 9.8 %custom-call.66 = f32[1,128,128]{1,2,0:T(8,128)S(1)} custom-call(f32[1,128,128]{2,1,0:T(8,128)S(1)} %get-tuple-element.340), custom_call_target="InvertDiagBlocksLowerTriangular" | custom-call | tf_op jit(solution)/shard_map/jit(cholesky)/cholesky | solution.py:52
  327.4 2.3 convolution_subtract_fusion.2
  329.8 12.1 %cholesky.487 = f32[128,128]{1,0:T(8,128)S(1)} custom-call(f32[128,128]{1,0:T(8,128)S(1)} %cholesky.594), custom_call_target="Cholesky" | custom-call | tf_op jit(solution)/shard_map/jit(cholesky)/cholesky | solution.py:52
  343.2 9.8 %custom-call.67 = f32[1,128,128]{1,2,0:T(8,128)S(1)} custom-call(f32[1,128,128]{2,1,0:T(8,128)S(1)} %get-tuple-element.337), custom_call_target="InvertDiagBlocksLowerTriangular" | custom-call | tf_op jit(solution)/shard_map/jit(cholesky)/cholesky | solution.py:52
  354.1 2.3 convolution_subtract_fusion.3
  356.4 11.7 %cholesky.506 = f32[128,128]{1,0:T(8,128)S(1)} custom-call(f32[128,128]{1,0:T(8,128)S(1)} %cholesky.599), custom_call_target="Cholesky" | custom-call | tf_op jit(solution)/shard_map/jit(cholesky)/cholesky | solution.py:52
  369.4 9.8 %custom-call.68 = f32[1,128,128]{1,2,0:T(8,128)S(1)} custom-call(f32[1,128,128]{2,1,0:T(8,128)S(1)} %get-tuple-element.334), custom_call_target="InvertDiagBlocksLowerTriangular" | custom-call | tf_op jit(solution)/shard_map/jit(cholesky)/cholesky | solution.py:52
  380.3 2.5 convolution_subtract_fusion.4
  382.8 11.7 %cholesky.526 = f32[128,128]{1,0:T(8,128)S(1)} custom-call(f32[128,128]{1,0:T(8,128)S(1)} %cholesky.604), custom_call_target="Cholesky" | custom-call | tf_op jit(solution)/shard_map/jit(cholesky)/cholesky | solution.py:52
  395.7 9.8 %custom-call.69 = f32[1,128,128]{1,2,0:T(8,128)S(1)} custom-call(f32[1,128,128]{2,1,0:T(8,128)S(1)} %get-tuple-element.331), custom_call_target="InvertDiagBlocksLowerTriangular" | custom-call | tf_op jit(solution)/shard_map/jit(cholesky)/cholesky | solution.py:52
  406.5 2.0 convolution_subtract_fusion.5
  408.5 11.7 %cholesky.546 = f32[128,128]{1,0:T(8,128)S(1)} custom-call(f32[128,128]{1,0:T(8,128)S(1)} %cholesky.609), custom_call_target="Cholesky" | custom-call | tf_op jit(solution)/shard_map/jit(cholesky)/cholesky | solution.py:52
  421.5 10.0 %custom-call.70 = f32[1,128,128]{1,2,0:T(8,128)S(1)} custom-call(f32[1,128,128]{2,1,0:T(8,128)S(1)} %get-tuple-element.328), custom_call_target="InvertDiagBlocksLowerTriangular" | custom-call | tf_op jit(solution)/shard_map/jit(cholesky)/cholesky | solution.py:52
  432.3 1.8 convolution_subtract_fusion.6
  434.1 11.7 %cholesky.564 = f32[128,128]{1,0:T(8,128)S(1)} custom-call(f32[128,128]{1,0:T(8,128)S(1)} %convolution_subtract_fusion.6), custom_call_target="Cholesky" | custom-call | tf_op jit(solution)/shard_map/jit(cholesky)/cholesky | solution.py:52
  452.8 4.8 select_select_fusion
  457.6 23.0 %while.38 = (s32[]{:T(128)}, f32[1024,1024]{1,0:T(8,128)}, s32[8,2]{0,1:T(2,128)S(1)}, f32[8,128,128]{2,1,0:T(8,128)S(1)}, s32[]{:T(128)}) while((s32[]{:T(128)}, f32[1024,1024]{1,0:T(8,128)}, s32[8,2]{0,1:T(2,128)S(1)}, f32[8,128,128]{2,1,0:T(8,128)S(1)}, s32[]{:T(128)}) %tuple.182), condition=%wide.while_cond, body=%wide.while_body.sunk | while | flops 2 | bytes 131181 | solution.py:57
  458.2 2.3 bitcast_dynamic-update-slice_fusion.2
  461.1 2.3 bitcast_dynamic-update-slice_fusion.2
  464.0 2.3 bitcast_dynamic-update-slice_fusion.2
  466.8 2.3 bitcast_dynamic-update-slice_fusion.2
  469.7 2.3 bitcast_dynamic-update-slice_fusion.2
  472.6 2.3 bitcast_dynamic-update-slice_fusion.2
  475.5 2.3 bitcast_dynamic-update-slice_fusion.2
  478.4 2.2 bitcast_dynamic-update-slice_fusion.2
  480.6 78.8 %custom-call.74 = f32[8,128,128]{1,2,0:T(8,128)S(1)} custom-call(f32[8,128,128]{2,1,0:T(8,128)S(1)} %get-tuple-element.269), custom_call_target="InvertDiagBlocksLowerTriangular" | custom-call | tf_op jit(solution)/shard_map/jit(_cho_solve)/triangular_solve | solution.py:57
  563.6 1.3 convolution_subtract_fusion.21
  565.1 1.4 convolution_subtract_fusion.36
  566.7 1.5 convolution_subtract_fusion.35
  568.4 1.6 convolution_subtract_fusion.34
  577.6 1.3 convolution_subtract_fusion.32
  579.2 1.4 convolution_subtract_fusion.31
  582.0 20.4 %all_gather.10 = f32[35,2048]{1,0:T(8,128)S(1)} all-gather(f32[35,128]{1,0:T(8,128)S(1)} %pad_maximum_fusion.1), channel_id=1, replica_groups=mesh['groups'=2,'pts'=8,'lm'=2] {'pts','lm'}, dimensions={1}, use_global_device_ids=true | all-gather | bytes 304640 | tf_op jit(solution)/shard_map/all_gather | solution.py:61
  602.5 2.7 while.36
  605.3 1.6 fusion.101
  606.9 30.1 %all-reduce.2 = (f32[32]{0:T(128)S(1)}, f32[32]{0:T(128)S(1)}) all-reduce(f32[32]{0:T(128)S(1)} %get-tuple-element.277, f32[32]{0:T(128)S(1)} %get-tuple-element.276), channel_id=1, replica_groups=mesh['groups'=2,'pts'=8,'lm'=2] {'pts','lm'}, use_global_device_ids=true, to_apply=%region_20.22 | all-reduce | flops 64 | bytes 512 | tf_op jit(solution)/shard_map/psum | solution.py:64
  637.0 55.5 %all-reduce.7.cloned.1.call-done = f32[32,1024]{1,0:T(8,128)} async-done(((f32[32,1024]{1,0:T(8,128)}), f32[32,1024]{1,0:T(8,128)}) %all-reduce.7.cloned.1.call-update) | async-done | bytes 131088 | tf_op jit(solution)/shard_map/psum | solution.py:64
  699.2 1.4 convolution_subtract_fusion.30
  700.8 1.5 convolution_subtract_fusion.29
  702.5 1.6 convolution_subtract_fusion.28
  711.7 1.3 convolution_subtract_fusion.26
  713.3 1.4 convolution_subtract_fusion.25
  716.1 22.9 %all_gather.11 = f32[35,2048]{1,0:T(8,128)S(1)} all-gather(f32[35,128]{1,0:T(8,128)S(1)} %pad_maximum_fusion), channel_id=1, replica_groups=mesh['groups'=2,'pts'=8,'lm'=2] {'pts','lm'}, dimensions={1}, use_global_device_ids=true | all-gather | bytes 304640 | tf_op jit(solution)/shard_map/all_gather | solution.py:61
  739.0 2.7 while.37
  741.9 29.8 %all-reduce.1 = (f32[32]{0:T(128)S(1)}, f32[32]{0:T(128)S(1)}) all-reduce(f32[32]{0:T(128)S(1)} %get-tuple-element.275, f32[32]{0:T(128)S(1)} %get-tuple-element.274), channel_id=1, replica_groups=mesh['groups'=2,'pts'=8,'lm'=2] {'pts','lm'}, use_global_device_ids=true, to_apply=%region_27.29 | all-reduce | flops 64 | bytes 512 | tf_op jit(solution)/shard_map/psum | solution.py:64
  (197 shorter events, 63.1 us)
Async XLA Ops:
  7.2 220.3 %all-reduce.9.cloned.1.call-start = ((), (), s32[]{:S(2)}) async-start(), calls=%async_computation.1 | async-start | bytes 8650752 | tf_op jit(solution)/shard_map/psum | solution.py:50
  114.9 577.7 %all-reduce.7.cloned.1.call-start = ((), (), s32[]{:S(2)}) async-start(), calls=%async_computation | async-start | bytes 262144 | tf_op jit(solution)/shard_map/psum | solution.py:64
  247.8 1.9 copy-start
  452.8 106.7 %copy-start.1 = (f32[32,1024]{1,0:T(8,128)S(1)}, f32[32,1024]{1,0:T(8,128)}, u32[]{:S(2)}) copy-start(f32[32,1024]{1,0:T(8,128)} %get-tuple-element.307) | copy-start | bytes 393220
  565.1 16.9 %copy-start.2 = (f32[3,128]{1,0:T(4,128)S(1)}, f32[3,128]{1,0:T(4,128)}, u32[]{:S(2)}) copy-start(f32[3,128]{1,0:T(4,128)} %param.10) | copy-start | bytes 4612
Sparse Core Ops, SparseCore 0:
  115.0 112.4 all-reduce.8
  607.0 85.4 all-reduce.6
where the time goes:
time: 789 us; the launch traced here: 780 us
  other arithmetic  276 us (35%)
  blocking collectives  193 us (24%)
  waiting for transfers between devices  168 us (21%)
  matrix products  81.6 us (10%)
  local copies, waits for them, and re-layouts  40.4 us (5%)
  between operations  20.6 us (3%)
    another operation x30, other arithmetic, body(): factor = jnp.linalg.cholesky(inner)  172 us
    psum x1, waiting for transfers between devices, body(): lax.psum(jnp.einsum('ri,rj->ij', cross, cross, precision=highest), ('pts'...  113 us
    another operation x4, other arithmetic, body(): weights = jax.scipy.linalg.cho_solve((factor, True), summed.T)  83.7 us
    psum x1, blocking collectives, body(): anchors = lax.psum(picked, ('pts', 'lm'))  68.3 us
    psum x2, blocking collectives, body(): lax.psum((jnp.sum(residual * scaled_res, axis=1), jnp.sum(scaled_res * im...  59.9 us
    psum x1, waiting for transfers between devices, body(): lax.psum((jnp.sum(residual * scaled_res, axis=1), jnp.sum(scaled_res * im...  55.5 us
    all_gather x2, blocking collectives, body(): lax.all_gather(stacked, ('pts', 'lm'), axis=1, tiled=True)  43.3 us
    another operation x60, matrix products, body(): weights = jax.scipy.linalg.cho_solve((factor, True), summed.T)  41.8 us
  transfers between devices with their start and end apart: 2, of which 2 were waited for; matrix products, arithmetic and copies ran while one was open for 0% of the time, Pallas kernels for 0%

commit v1 on v0

--- a/solution.py
+++ b/solution.py
@@ -45,7 +45,7 @@
     local = landmarks - offset
     inside = (local >= 0) & (local < rows)
     picked = jnp.where(inside[None, :], jnp.take(points, jnp.clip(local, 0, rows - 1), axis=1), 0.0)
-    anchors = lax.psum(picked, ("pts", "lm"))
+    anchors = jnp.sum(lax.all_gather(picked, ("pts", "lm")), axis=0)
     cross = matern(points, anchors)
     gram = lax.psum(jnp.einsum("ri,rj->ij", cross, cross, precision=highest), ("pts", "lm"))
     inner = matern(anchors, anchors) + jnp.eye(count, dtype=jnp.float32) + gram

time: 789 us -> 742 us (0.940)
  blocking collectives: 193 us -> 148 us
    psum x1 -> x0, blocking collectives: 68.3 us -> none  [body(): anchors = lax.psum(picked, ('pts', 'lm'))]
    all_gather x0 -> x1, blocking collectives: none -> 23.8 us  [body(): anchors = jnp.sum(lax.all_gather(picked, ('pts', 'lm')), axis=0)]
where the time goes in v1:
time: 742 us; the launch traced here: 733 us
  other arithmetic  276 us (37%)
  waiting for transfers between devices  167 us (23%)
  blocking collectives  148 us (20%)
  matrix products  81.2 us (11%)
  local copies, waits for them, and re-layouts  39.8 us (5%)
  between operations  20.6 us (3%)
    another operation x30, other arithmetic, body(): factor = jnp.linalg.cholesky(inner)  172 us
    psum x1, waiting for transfers between devices, body(): lax.psum(jnp.einsum('ri,rj->ij', cross, cross, precision=highest), ('pts'...  112 us
    another operation x4, other arithmetic, body(): weights = jax.scipy.linalg.cho_solve((factor, True), summed.T)  83.7 us
    psum x2, blocking collectives, body(): lax.psum((jnp.sum(residual * scaled_res, axis=1), jnp.sum(scaled_res * im...  59.9 us
    psum x1, waiting for transfers between devices, body(): lax.psum((jnp.sum(residual * scaled_res, axis=1), jnp.sum(scaled_res * im...  55.5 us
    all_gather x2, blocking collectives, body(): lax.all_gather(stacked, ('pts', 'lm'), axis=1, tiled=True)  43.3 us
    another operation x60, matrix products, body(): weights = jax.scipy.linalg.cho_solve((factor, True), summed.T)  41.4 us
    all_gather x1, blocking collectives, body(): anchors = jnp.sum(lax.all_gather(picked, ('pts', 'lm')), axis=0)  23.8 us
  transfers between devices with their start and end apart: 2, of which 2 were waited for; matrix products, arithmetic and copies ran while one was open for 0% of the time, Pallas kernels for 0%

profile of v1, /device:TPU:0, one launch (start us, length us, event | category | flops | bytes accessed | tf_op | source)
XLA Modules:
  0.0 732.8 jit_solution(5149334190683457857)
XLA Ops:
  11.5 2.8 gather_fusion.1
  14.9 23.8 %all_gather.14 = f32[16,3,1024]{2,1,0:T(4,128)S(1)} all-gather(f32[1,3,1024]{2,1,0:T(4,128)S(1)} %copy.21), channel_id=1, replica_groups=mesh['groups'=2,'pts'=8,'lm'=2] {'pts','lm'}, dimensions={0}, use_global_device_ids=true | all-gather | bytes 208896 | tf_op jit(solution)/shard_map/all_gather | solution.py:48
  39.6 20.5 %all_gather.13 = f32[32,2048]{0,1:T(8,128)S(1)} all-gather(f32[32,128]{0,1:T(8,128)S(1)} %copy.18), channel_id=1, replica_groups=mesh['groups'=2,'pts'=8,'lm'=2] {'pts','lm'}, dimensions={1}, use_global_device_ids=true | all-gather | bytes 278528 | tf_op jit(solution)/shard_map/all_gather | solution.py:43
  60.8 6.6 fusion.104
  67.4 1.6 fusion.103
  69.1 111.8 %all-reduce.9.cloned.1.call-done = (f32[1024,1024]{0,1:T(8,128)}, f32[32,1024]{1,0:T(8,128)}) async-done(((f32[1024,1024]{0,1:T(8,128)}, f32[32,1024]{1,0:T(8,128)}), (f32[1024,1024]{0,1:T(8,128)}, f32[32,1024]{1,0:T(8,128)})) %all-reduce.9.cloned.1.call-update) | async-done | bytes 4325392 | tf_op jit(solution)/shard_map/psum | solution.py:50
  180.9 7.6 %add_add_fusion = f32[1024,1024]{0,1:T(8,128)} fusion(f32[1024,1024]{0,1:T(8,128)} %get-tuple-element.303, f32[1024]{0:T(1024)S(1)} %bitcast.288, f32[1024]{0:T(1024)S(1)} %bitcast.281, f32[1024]{0:T(1024)S(1)} %bitcast.274), kind=kLoop, calls=%fused_computation.92 | loop fusion | flops 20971520 | bytes 8400896 | tf_op jit(solution)/shard_map/add | solution.py:51
  188.5 5.3 copy.24
  193.8 7.4 %fusion.74 = f32[1024,1024]{1,0:T(8,128)S(1)} fusion(f32[1024,1024]{1,0:T(8,128)} %copy.24, f32[1024,1024]{0,1:T(8,128)} %get-tuple-element.303, f32[1024]{0:T(1024)S(1)} %bitcast.289, f32[1024]{0:T(1024)S(1)} %bitcast.282, f32[1024]{0:T(1024)S(1)} %bitcast.275), kind=kLoop, calls=%fused_computation.90 | loop fusion | flops 23068672 | bytes 12595200 | tf_op jit(solution)/shard_map/jit(cholesky)/div | solution.py:52
  201.2 1.9 copy-done
  203.1 11.7 %cholesky.223 = f32[128,128]{1,0:T(8,128)S(1)} custom-call(f32[128,128]{1,0:T(8,128)S(1)} %cholesky.580), custom_call_target="Cholesky" | custom-call | tf_op jit(solution)/shard_map/jit(cholesky)/cholesky | solution.py:52
  214.9 2.5 cholesky.255
  217.4 9.8 %custom-call.64 = f32[1,128,128]{1,2,0:T(8,128)S(1)} custom-call(f32[1,128,128]{2,1,0:T(8,128)S(1)} %get-tuple-element.343), custom_call_target="InvertDiagBlocksLowerTriangular" | custom-call | tf_op jit(solution)/shard_map/jit(cholesky)/cholesky | solution.py:52
  227.2 2.4 constant_dynamic-update-slice_fusion.93
  229.6 1.5 convolution_subtract_fusion
  231.1 11.7 %cholesky.244 = f32[128,128]{1,0:T(8,128)S(1)} custom-call(f32[128,128]{1,0:T(8,128)S(1)} %cholesky.584), custom_call_target="Cholesky" | custom-call | tf_op jit(solution)/shard_map/jit(cholesky)/cholesky | solution.py:52
  243.5 10.0 %custom-call.65 = f32[1,128,128]{1,2,0:T(8,128)S(1)} custom-call(f32[1,128,128]{2,1,0:T(8,128)S(1)} %get-tuple-element.340), custom_call_target="InvertDiagBlocksLowerTriangular" | custom-call | tf_op jit(solution)/shard_map/jit(cholesky)/cholesky | solution.py:52
  254.7 2.1 convolution_subtract_fusion.1
  256.9 11.7 %cholesky.468 = f32[128,128]{1,0:T(8,128)S(1)} custom-call(f32[128,128]{1,0:T(8,128)S(1)} %cholesky.589), custom_call_target="Cholesky" | custom-call | tf_op jit(solution)/shard_map/jit(cholesky)/cholesky | solution.py:52
  269.8 9.8 %custom-call.66 = f32[1,128,128]{1,2,0:T(8,128)S(1)} custom-call(f32[1,128,128]{2,1,0:T(8,128)S(1)} %get-tuple-element.337), custom_call_target="InvertDiagBlocksLowerTriangular" | custom-call | tf_op jit(solution)/shard_map/jit(cholesky)/cholesky | solution.py:52
  280.8 2.3 convolution_subtract_fusion.2
  283.1 12.1 %cholesky.487 = f32[128,128]{1,0:T(8,128)S(1)} custom-call(f32[128,128]{1,0:T(8,128)S(1)} %cholesky.594), custom_call_target="Cholesky" | custom-call | tf_op jit(solution)/shard_map/jit(cholesky)/cholesky | solution.py:52
  296.5 9.8 %custom-call.67 = f32[1,128,128]{1,2,0:T(8,128)S(1)} custom-call(f32[1,128,128]{2,1,0:T(8,128)S(1)} %get-tuple-element.334), custom_call_target="InvertDiagBlocksLowerTriangular" | custom-call | tf_op jit(solution)/shard_map/jit(cholesky)/cholesky | solution.py:52
  307.5 2.3 convolution_subtract_fusion.3
  309.8 11.7 %cholesky.506 = f32[128,128]{1,0:T(8,128)S(1)} custom-call(f32[128,128]{1,0:T(8,128)S(1)} %cholesky.599), custom_call_target="Cholesky" | custom-call | tf_op jit(solution)/shard_map/jit(cholesky)/cholesky | solution.py:52
  322.8 9.8 %custom-call.68 = f32[1,128,128]{1,2,0:T(8,128)S(1)} custom-call(f32[1,128,128]{2,1,0:T(8,128)S(1)} %get-tuple-element.331), custom_call_target="InvertDiagBlocksLowerTriangular" | custom-call | tf_op jit(solution)/shard_map/jit(cholesky)/cholesky | solution.py:52
  333.7 2.5 convolution_subtract_fusion.4
  336.1 11.7 %cholesky.526 = f32[128,128]{1,0:T(8,128)S(1)} custom-call(f32[128,128]{1,0:T(8,128)S(1)} %cholesky.604), custom_call_target="Cholesky" | custom-call | tf_op jit(solution)/shard_map/jit(cholesky)/cholesky | solution.py:52
  349.1 9.8 %custom-call.69 = f32[1,128,128]{1,2,0:T(8,128)S(1)} custom-call(f32[1,128,128]{2,1,0:T(8,128)S(1)} %get-tuple-element.328), custom_call_target="InvertDiagBlocksLowerTriangular" | custom-call | tf_op jit(solution)/shard_map/jit(cholesky)/cholesky | solution.py:52
  359.9 2.0 convolution_subtract_fusion.5
  361.9 11.7 %cholesky.546 = f32[128,128]{1,0:T(8,128)S(1)} custom-call(f32[128,128]{1,0:T(8,128)S(1)} %cholesky.609), custom_call_target="Cholesky" | custom-call | tf_op jit(solution)/shard_map/jit(cholesky)/cholesky | solution.py:52
  374.9 10.0 %custom-call.70 = f32[1,128,128]{1,2,0:T(8,128)S(1)} custom-call(f32[1,128,128]{2,1,0:T(8,128)S(1)} %get-tuple-element.325), custom_call_target="InvertDiagBlocksLowerTriangular" | custom-call | tf_op jit(solution)/shard_map/jit(cholesky)/cholesky | solution.py:52
  385.7 1.8 convolution_subtract_fusion.6
  387.5 11.7 %cholesky.564 = f32[128,128]{1,0:T(8,128)S(1)} custom-call(f32[128,128]{1,0:T(8,128)S(1)} %convolution_subtract_fusion.6), custom_call_target="Cholesky" | custom-call | tf_op jit(solution)/shard_map/jit(cholesky)/cholesky | solution.py:52
  406.2 4.8 select_select_fusion
  411.0 23.0 %while.38 = (s32[]{:T(128)}, f32[1024,1024]{1,0:T(8,128)}, s32[8,2]{0,1:T(2,128)S(1)}, f32[8,128,128]{2,1,0:T(8,128)S(1)}, s32[]{:T(128)}) while((s32[]{:T(128)}, f32[1024,1024]{1,0:T(8,128)}, s32[8,2]{0,1:T(2,128)S(1)}, f32[8,128,128]{2,1,0:T(8,128)S(1)}, s32[]{:T(128)}) %tuple.182), condition=%wide.while_cond, body=%wide.while_body.sunk | while | flops 2 | bytes 131181 | solution.py:57
  411.6 2.3 bitcast_dynamic-update-slice_fusion.2
  414.5 2.3 bitcast_dynamic-update-slice_fusion.2
  417.3 2.3 bitcast_dynamic-update-slice_fusion.2
  420.2 2.3 bitcast_dynamic-update-slice_fusion.2
  423.1 2.3 bitcast_dynamic-update-slice_fusion.2
  426.0 2.3 bitcast_dynamic-update-slice_fusion.2
  428.9 2.3 bitcast_dynamic-update-slice_fusion.2
  431.8 2.2 bitcast_dynamic-update-slice_fusion.2
  434.0 78.8 %custom-call.74 = f32[8,128,128]{1,2,0:T(8,128)S(1)} custom-call(f32[8,128,128]{2,1,0:T(8,128)S(1)} %get-tuple-element.269), custom_call_target="InvertDiagBlocksLowerTriangular" | custom-call | tf_op jit(solution)/shard_map/jit(_cho_solve)/triangular_solve | solution.py:57
  517.0 1.3 convolution_subtract_fusion.21
  518.5 1.4 convolution_subtract_fusion.36
  520.1 1.5 convolution_subtract_fusion.35
  521.8 1.6 convolution_subtract_fusion.34
  530.8 1.3 convolution_subtract_fusion.32
  532.4 1.4 convolution_subtract_fusion.31
  535.3 20.4 %all_gather.15 = f32[35,2048]{1,0:T(8,128)S(1)} all-gather(f32[35,128]{1,0:T(8,128)S(1)} %pad_maximum_fusion.1), channel_id=1, replica_groups=mesh['groups'=2,'pts'=8,'lm'=2] {'pts','lm'}, dimensions={1}, use_global_device_ids=true | all-gather | bytes 304640 | tf_op jit(solution)/shard_map/all_gather | solution.py:61
  555.7 2.7 while.36
  558.6 1.6 fusion.102
  560.2 30.1 %all-reduce.2 = (f32[32]{0:T(128)S(1)}, f32[32]{0:T(128)S(1)}) all-reduce(f32[32]{0:T(128)S(1)} %get-tuple-element.274, f32[32]{0:T(128)S(1)} %get-tuple-element.273), channel_id=1, replica_groups=mesh['groups'=2,'pts'=8,'lm'=2] {'pts','lm'}, use_global_device_ids=true, to_apply=%region_20.22 | all-reduce | flops 64 | bytes 512 | tf_op jit(solution)/shard_map/psum | solution.py:64
  590.3 55.5 %all-reduce.7.cloned.1.call-done = f32[32,1024]{1,0:T(8,128)} async-done(((f32[32,1024]{1,0:T(8,128)}), f32[32,1024]{1,0:T(8,128)}) %all-reduce.7.cloned.1.call-update) | async-done | bytes 131088 | tf_op jit(solution)/shard_map/psum | solution.py:64
  652.4 1.4 convolution_subtract_fusion.30
  654.1 1.5 convolution_subtract_fusion.29
  655.7 1.6 convolution_subtract_fusion.28
  664.7 1.3 convolution_subtract_fusion.26
  666.4 1.4 convolution_subtract_fusion.25
  669.2 22.9 %all_gather.16 = f32[35,2048]{1,0:T(8,128)S(1)} all-gather(f32[35,128]{1,0:T(8,128)S(1)} %pad_maximum_fusion), channel_id=1, replica_groups=mesh['groups'=2,'pts'=8,'lm'=2] {'pts','lm'}, dimensions={1}, use_global_device_ids=true | all-gather | bytes 304640 | tf_op jit(solution)/shard_map/all_gather | solution.py:61
  692.0 2.7 while.37
  695.0 29.8 %all-reduce.1 = (f32[32]{0:T(128)S(1)}, f32[32]{0:T(128)S(1)}) all-reduce(f32[32]{0:T(128)S(1)} %get-tuple-element.272, f32[32]{0:T(128)S(1)} %get-tuple-element.271), channel_id=1, replica_groups=mesh['groups'=2,'pts'=8,'lm'=2] {'pts','lm'}, use_global_device_ids=true, to_apply=%region_27.29 | all-reduce | flops 64 | bytes 512 | tf_op jit(solution)/shard_map/psum | solution.py:64
  (199 shorter events, 62.3 us)
Async XLA Ops:
  7.2 173.7 %all-reduce.9.cloned.1.call-start = ((), (), s32[]{:S(2)}) async-start(), calls=%async_computation.1 | async-start | bytes 8650752 | tf_op jit(solution)/shard_map/psum | solution.py:50
  69.0 576.8 %all-reduce.7.cloned.1.call-start = ((), (), s32[]{:S(2)}) async-start(), calls=%async_computation | async-start | bytes 262144 | tf_op jit(solution)/shard_map/psum | solution.py:64
  201.2 1.9 copy-start
  406.1 106.7 %copy-start.1 = (f32[32,1024]{1,0:T(8,128)S(1)}, f32[32,1024]{1,0:T(8,128)}, u32[]{:S(2)}) copy-start(f32[32,1024]{1,0:T(8,128)} %get-tuple-element.304) | copy-start | bytes 393220
  518.5 16.7 %copy-start.2 = (f32[3,128]{1,0:T(4,128)S(1)}, f32[3,128]{1,0:T(4,128)}, u32[]{:S(2)}) copy-start(f32[3,128]{1,0:T(4,128)} %param.10) | copy-start | bytes 4612
Sparse Core Ops, SparseCore 0:
  69.1 111.6 all-reduce.8
  560.3 85.4 all-reduce.6
